TPU v7x, 128 devices: a whole 4x4x4 slice. The times are simulated.
128 devices in a mesh: rows: 8 (over y_hi, z), bundle: 16 (over y_lo, x, core).
Axes of the slice: x: 4, y: 4 (y_hi: 2, y_lo: 2; y = y_hi * 2 + y_lo), z: 4, core: 2. Of those that a mesh axis runs over, the one named last changes fastest.
Arguments:
- raw_values: float32 [32768, 4096], P(('rows', 'bundle')), may hold values from -2100 to 2100
- bin_edges: float32 [4096, 255], P(('rows', 'bundle')), may hold values from -2100 to 2100, as said below
- feature_column: int32 [4096], replicated, may hold values from 0 to 4095, each once
- bin_offset: int32 [4096], replicated, may hold values from 0 to 63
Outputs:
- bin_codes: int32 [32768, 4096], P('rows', 'bundle')
Inputs may be any that keep to these rules, and one draw needn't show every extreme that they name: Every row of bin_edges is strictly increasing. `feature_column`: each column 0 .. 4095 is named once.
All inputs are finite; a program needn't handle non-finite values.
Results may differ from a plain program's by a relative error of at most 0.0003.
Values may be sent and summed in bfloat16 or wider, within the bound.
No kernel may reach another device: no remote copies, remote signals or barrier semaphores. Data moves between devices by JAX's collectives and lax.ppermute only.
A program may use at most 64 MiB of HBM per device.

v0:
```python
import math
import jax
import jax.numpy as jnp
from jax import lax
from jax.sharding import PartitionSpec as P


def count_below(values, edges):
    total = values.shape[0]
    block = math.gcd(total, 512)

    def one_block(part_rows):
        return jnp.sum(part_rows[:, :, None] > edges[None, :, :], axis=2, dtype=jnp.int32)

    blocks = values.reshape(total // block, block, values.shape[1])
    return lax.map(one_block, blocks).reshape(total, values.shape[1])


def local(raw_values, bin_edges, feature_column, bin_offset):
    count_feat = feature_column.shape[0]
    owner_feature = (
        jnp.zeros((count_feat,), jnp.int32)
        .at[feature_column]
        .set(jnp.arange(count_feat, dtype=jnp.int32))
    )
    edges_all = lax.all_gather(bin_edges, ("rows", "bundle"), axis=0, tiled=True)
    span_cols = count_feat // lax.axis_size("bundle")
    first_col = lax.axis_index("bundle") * span_cols
    owned_features = lax.dynamic_slice_in_dim(owner_feature, first_col, span_cols, 0)
    owned_offsets = jnp.take(bin_offset, owned_features)
    ordered = jnp.take(raw_values, owner_feature, axis=1)
    arrived = lax.all_to_all(ordered, "bundle", split_axis=1, concat_axis=0, tiled=True)
    owned_edges = jnp.take(edges_all, owned_features, axis=0)
    bins = count_below(arrived, owned_edges)
    return bins + owned_offsets[None, :]


def solution(mesh):
    in_specs = (P(("rows", "bundle"), None), P(("rows", "bundle"), None), P(), P())
    out_specs = P("rows", "bundle")
    return jax.shard_map(local, mesh=mesh, in_specs=in_specs, out_specs=out_specs, check_vma=False)
```

profile of v0, /device:TPU:1, one launch (start us, length us, event | category | flops | bytes accessed | tf_op | source)
XLA Modules:
  0.0 402.5 jit_solution(2743902135054900471)
XLA Ops:
  7.3 5.6 %copy.9 = f32[256,4096]{0,1:T(8,128)} copy(f32[256,4096]{1,0:T(8,128)} %param.6) | data formatting | bytes 8388608 | tf_op args[0]
  12.9 15.5 %scatter_custom_fusion = s32[4096]{0:T(1024)S(1)} fusion(s32[4096]{0:T(1024)S(1)} %compare_select_fusion.1, s32[4096]{0:T(1024)S(1)} %iota.3, s32[]{:T(128)} %copy.20), kind=kCustom, calls=%fused_computation.14 | custom fusion | bytes 16388 | tf_op jit(solution)/shard_map/scatter | solution.py:24
  28.5 18.4 %gather_fusion = f32[4096,256]{1,0:T(8,128)} fusion(f32[256,4096]{0,1:T(8,128)} %copy.9, s32[4096]{0:T(1024)S(1)} %fusion), kind=kCustom, calls=%fused_computation | custom fusion | bytes 8404992 | tf_op jit(solution)/shard_map/jit(_take)/gather | solution.py:31
  46.9 3.9 broadcast_select_fusion
  50.8 6.8 %all-to-all-start = ((f32[256,16,256]{0,2,1:T(8,128)}), f32[256,16,256]{0,2,1:T(8,128)}, u32[]{:S(2)}, u32[]{:S(2)}) async-start(f32[256,16,256]{0,2,1:T(8,128)} %broadcast_select_fusion), calls=%async_computation | async-start | bytes 8388608 | tf_op jit(solution)/shard_map/all_to_all | solution.py:32
  57.7 1.7 gather_fusion.2
  59.5 55.1 %all-to-all-done = f32[256,16,256]{0,2,1:T(8,128)} async-done(((f32[256,16,256]{0,2,1:T(8,128)}), f32[256,16,256]{0,2,1:T(8,128)}, u32[]{:S(2)}, u32[]{:S(2)}) %all-to-all-start) | async-done | bytes 4194336 | tf_op jit(solution)/shard_map/all_to_all | solution.py:32
  114.6 5.3 %copy.10 = f32[16,256,256]{2,1,0:T(8,128)} copy(f32[16,256,256]{1,2,0:T(8,128)} %bitcast.4) | data formatting | bytes 8388608 | tf_op jit(solution)/shard_map/all_to_all | solution.py:32
  119.9 122.6 %all-gather.2.cloned.1.call-done = f32[4096,255]{1,0:T(8,128)} async-done(((f32[32,255]{1,0:T(8,128)}), f32[4096,255]{1,0:T(8,128)}) %all-gather.2.cloned.1.call-update) | async-done | bytes 4177936 | tf_op jit(solution)/shard_map/all_gather | solution.py:26
  242.6 3.2 gather_fusion.1
  246.0 145.3 %while.10 = (s32[]{:T(128)}, s32[8,512,256]{2,1,0:T(8,128)}, f32[8,512,256]{2,1,0:T(8,128)}, f32[256,255]{0,1:T(8,128)S(1)}, s32[]{:T(128)}) while((s32[]{:T(128)}, s32[8,512,256]{2,1,0:T(8,128)}, f32[8,512,256]{2,1,0:T(8,128)}, f32[256,255]{0,1:T(8,128)S(1)}, s32[]{:T(128)}) %tuple.25), condition=%wide.region_3.4_spmd, body=%wide.region_1.0_spmd.sunk | while | flops 100139008 | bytes 3407425 | solution.py:16
  246.0 1.1 dynamic-slice_bitcast_fusion.2
  247.1 16.2 %convert_reduce_fusion.2 = s32[512,256]{1,0:T(8,128)S(1)} fusion(f32[256,255]{0,1:T(8,128)S(1)} %get-tuple-element.80, f32[512,256]{1,0:T(8,128)S(1)} %dynamic-slice_bitcast_fusion.2), kind=kLoop, calls=%fused_computation.4.clone.1 | loop fusion | flops 100139008 | bytes 1309696 | tf_op jit(solution)/shard_map/while/body/eval_jaxpr/reduce_sum | solution.py:13
  264.1 1.1 dynamic-slice_bitcast_fusion.2
  265.2 16.2 %convert_reduce_fusion.2 = s32[512,256]{1,0:T(8,128)S(1)} fusion(f32[256,255]{0,1:T(8,128)S(1)} %get-tuple-element.80, f32[512,256]{1,0:T(8,128)S(1)} %dynamic-slice_bitcast_fusion.2), kind=kLoop, calls=%fused_computation.4.clone.1 | loop fusion | flops 100139008 | bytes 1309696 | tf_op jit(solution)/shard_map/while/body/eval_jaxpr/reduce_sum | solution.py:13
  282.3 1.1 dynamic-slice_bitcast_fusion.2
  283.4 16.2 %convert_reduce_fusion.2 = s32[512,256]{1,0:T(8,128)S(1)} fusion(f32[256,255]{0,1:T(8,128)S(1)} %get-tuple-element.80, f32[512,256]{1,0:T(8,128)S(1)} %dynamic-slice_bitcast_fusion.2), kind=kLoop, calls=%fused_computation.4.clone.1 | loop fusion | flops 100139008 | bytes 1309696 | tf_op jit(solution)/shard_map/while/body/eval_jaxpr/reduce_sum | solution.py:13
  300.5 1.1 dynamic-slice_bitcast_fusion.2
  301.5 16.2 %convert_reduce_fusion.2 = s32[512,256]{1,0:T(8,128)S(1)} fusion(f32[256,255]{0,1:T(8,128)S(1)} %get-tuple-element.80, f32[512,256]{1,0:T(8,128)S(1)} %dynamic-slice_bitcast_fusion.2), kind=kLoop, calls=%fused_computation.4.clone.1 | loop fusion | flops 100139008 | bytes 1309696 | tf_op jit(solution)/shard_map/while/body/eval_jaxpr/reduce_sum | solution.py:13
  319.7 16.2 %convert_reduce_fusion.2 = s32[512,256]{1,0:T(8,128)S(1)} fusion(f32[256,255]{0,1:T(8,128)S(1)} %get-tuple-element.80, f32[512,256]{1,0:T(8,128)S(1)} %dynamic-slice_bitcast_fusion.2), kind=kLoop, calls=%fused_computation.4.clone.1 | loop fusion | flops 100139008 | bytes 1309696 | tf_op jit(solution)/shard_map/while/body/eval_jaxpr/reduce_sum | solution.py:13
  337.8 16.2 %convert_reduce_fusion.2 = s32[512,256]{1,0:T(8,128)S(1)} fusion(f32[256,255]{0,1:T(8,128)S(1)} %get-tuple-element.80, f32[512,256]{1,0:T(8,128)S(1)} %dynamic-slice_bitcast_fusion.2), kind=kLoop, calls=%fused_computation.4.clone.1 | loop fusion | flops 100139008 | bytes 1309696 | tf_op jit(solution)/shard_map/while/body/eval_jaxpr/reduce_sum | solution.py:13
  356.0 16.2 %convert_reduce_fusion.2 = s32[512,256]{1,0:T(8,128)S(1)} fusion(f32[256,255]{0,1:T(8,128)S(1)} %get-tuple-element.80, f32[512,256]{1,0:T(8,128)S(1)} %dynamic-slice_bitcast_fusion.2), kind=kLoop, calls=%fused_computation.4.clone.1 | loop fusion | flops 100139008 | bytes 1309696 | tf_op jit(solution)/shard_map/while/body/eval_jaxpr/reduce_sum | solution.py:13
  374.1 16.2 %convert_reduce_fusion.2 = s32[512,256]{1,0:T(8,128)S(1)} fusion(f32[256,255]{0,1:T(8,128)S(1)} %get-tuple-element.80, f32[512,256]{1,0:T(8,128)S(1)} %dynamic-slice_bitcast_fusion.2), kind=kLoop, calls=%fused_computation.4.clone.1 | loop fusion | flops 100139008 | bytes 1309696 | tf_op jit(solution)/shard_map/while/body/eval_jaxpr/reduce_sum | solution.py:13
  391.2 4.5 %bitcast_add_fusion = s32[4096,256]{1,0:T(8,128)} fusion(s32[8,512,256]{2,1,0:T(8,128)} %get-tuple-element.27, s32[256]{0:T(256)S(1)} %get-tuple-element.40), kind=kLoop, calls=%fused_computation.7 | loop fusion | flops 1048576 | bytes 8389632 | tf_op jit(solution)/shard_map/add | solution.py:35
  (29 shorter events, 12.2 us)
Async XLA Ops:
  6.5 51.2 %copy-start = (s32[4096]{0:T(1024)S(1)}, s32[4096]{0:T(1024)}, u32[]{:S(2)}) copy-start(s32[4096]{0:T(1024)} %param.9) | copy-start | bytes 49156
  6.5 236.0 %all-gather.2.cloned.1.call-start = ((), (), s32[]{:S(2)}) async-start(), calls=%async_computation.1 | async-start | bytes 4227072 | tf_op jit(solution)/shard_map/all_gather | solution.py:26
  7.3 5.6 %copy-start.1 = (s32[4096]{0:T(1024)S(1)}, s32[4096]{0:T(1024)}, u32[]{:S(2)}) copy-start(s32[4096]{0:T(1024)} %param.8) | copy-start | bytes 49156
  50.8 63.8 %all-to-all-start = ((f32[256,16,256]{0,2,1:T(8,128)}), f32[256,16,256]{0,2,1:T(8,128)}, u32[]{:S(2)}, u32[]{:S(2)}) async-start(f32[256,16,256]{0,2,1:T(8,128)} %broadcast_select_fusion), calls=%async_computation | async-start | bytes 8388608 | tf_op jit(solution)/shard_map/all_to_all | solution.py:32
Sparse Core Ops, SparseCore 0:
  9.1 233.4 all-gather.1
where the time goes:
time: 403 us
  waiting for transfers between devices  178 us (44%)
  other arithmetic  139 us (34%)
  local copies, waits for them, and re-layouts  65.2 us (16%)
  between operations  13.5 us (3%)
  starting transfers between devices  6.83 us (2%)
    reduce_sum x8, other arithmetic, one_block(): jnp.sum(part_rows[:, :, None] > edges[None, :, :], axis=2, dtype=jnp.int32)  130 us
    all_gather x1, waiting for transfers between devices, local(): lax.all_gather(bin_edges, ('rows', 'bundle'), axis=0, tiled=True)  123 us
    all_to_all x1, waiting for transfers between devices, local(): lax.all_to_all(ordered, 'bundle', split_axis=1, concat_axis=0, tiled=True)  55.1 us
    gather x1, local copies, waits for them, and re-layouts, local(): ordered = jnp.take(raw_values, owner_feature, axis=1)  18.4 us
    scatter x1, local copies, waits for them, and re-layouts, local(): owner_feature = jnp.zeros((count_feat,), jnp.int32).at[feature_column].se...  15.5 us
    gt x8, local copies, waits for them, and re-layouts, one_block(): part_rows[:, :, None] > edges[None, :, :]  8.61 us
  transfers between devices with their start and end apart: 2, of which 2 were waited for; matrix products, arithmetic and copies ran while one was open for 13% of the time, Pallas kernels for 0%

commit v1 on v0

--- a/solution.py
+++ b/solution.py
@@ -23,7 +23,12 @@
         .at[feature_column]
         .set(jnp.arange(count_feat, dtype=jnp.int32))
     )
-    edges_all = lax.all_gather(bin_edges, ("rows", "bundle"), axis=0, tiled=True)
+    edges_all = jnp.concatenate(
+        lax.all_to_all(
+            jnp.stack([bin_edges] * lax.axis_size(("rows", "bundle"))), ("rows", "bundle"), 0, 0
+        ),
+        axis=0,
+    )
     span_cols = count_feat // lax.axis_size("bundle")
     first_col = lax.axis_index("bundle") * span_cols
     owned_features = lax.dynamic_slice_in_dim(owner_feature, first_col, span_cols, 0)

time: 403 us -> 317 us (0.79)
  waiting for transfers between devices: 178 us -> 45.1 us
  blocking collectives: 0 us -> 55.5 us
  between operations: 13.5 us -> 0.1 us
    all_gather x1 -> x0, waiting for transfers between devices: 123 us -> none  [local(): lax.all_gather(bin_edges, ('rows', 'bundle'), axis=0, tiled=True)]
    all_to_all x0 -> x1, blocking collectives: none -> 55.5 us  [local(): lax.all_to_all(ordered, 'bundle', split_axis=1, concat_axis=0, tiled=True)]
    all_to_all x1, waiting for transfers between devices: 55.1 us -> 45.1 us  [local(): lax.all_to_all(jnp.stack([bin_edges] * lax.axis_size(('rows', 'bundle')))...]
  transfers between devices with their start and end apart: 2 -> 1, of which waited for: 2 -> 1; matrix products, arithmetic and copies ran while one was open for 13% -> 2% of each run, Pallas kernels for 0% -> 0%
where the time goes in v1:
time: 317 us; the launch traced here: 316 us
  other arithmetic  139 us (44%)
  local copies, waits for them, and re-layouts  67.5 us (21%)
  blocking collectives  55.5 us (18%)
  waiting for transfers between devices  45.1 us (14%)
  starting transfers between devices  9.13 us (3%)
    reduce_sum x8, other arithmetic, one_block(): jnp.sum(part_rows[:, :, None] > edges[None, :, :], axis=2, dtype=jnp.int32)  130 us
    all_to_all x1, blocking collectives, local(): lax.all_to_all(ordered, 'bundle', split_axis=1, concat_axis=0, tiled=True)  55.5 us
    all_to_all x1, waiting for transfers between devices, local(): lax.all_to_all(jnp.stack([bin_edges] * lax.axis_size(('rows', 'bundle')))...  45.1 us
    gather x1, local copies, waits for them, and re-layouts, local(): ordered = jnp.take(raw_values, owner_feature, axis=1)  18.3 us
    scatter x1, local copies, waits for them, and re-layouts, local(): owner_feature = jnp.zeros((count_feat,), jnp.int32).at[feature_column].se...  15.5 us
    all_to_all x1, starting transfers between devices, local(): lax.all_to_all(jnp.stack([bin_edges] * lax.axis_size(('rows', 'bundle')))...  9.13 us
    gt x8, local copies, waits for them, and re-layouts, one_block(): part_rows[:, :, None] > edges[None, :, :]  8.61 us
    dynamic_update_slice x8, local copies, waits for them, and re-layouts, count_below(): return lax.map(one_block, blocks).reshape(total, values.shape[1])  6.68 us
  transfers between devices with their start and end apart: 1, of which 1 were waited for; matrix products, arithmetic and copies ran while one was open for 2% of the time, Pallas kernels for 0%

profile of v1, /device:TPU:1, one launch (start us, length us, event | category | flops | bytes accessed | tf_op | source)
XLA Modules:
  0.0 316.0 jit_solution(4781758298036527332)
XLA Ops:
  0.7 15.5 %scatter_custom_fusion = s32[4096]{0:T(1024)S(1)} fusion(s32[4096]{0:T(1024)S(1)} %compare_select_fusion.1, s32[4096]{0:T(1024)S(1)} %iota.3, s32[]{:T(128)} %copy.20), kind=kCustom, calls=%fused_computation.14 | custom fusion | bytes 16388 | tf_op jit(solution)/shard_map/scatter | solution.py:24
  16.3 5.6 %copy.9 = f32[256,4096]{0,1:T(8,128)} copy(f32[256,4096]{1,0:T(8,128)} %param.6) | data formatting | bytes 8388608 | tf_op args[0]
  21.9 18.3 %gather_fusion = f32[4096,256]{1,0:T(8,128)} fusion(f32[256,4096]{0,1:T(8,128)} %copy.9, s32[4096]{0:T(1024)S(1)} %fusion), kind=kCustom, calls=%fused_computation | custom fusion | bytes 8404992 | tf_op jit(solution)/shard_map/jit(_take)/gather | solution.py:36
  40.2 3.3 %broadcast_select_fusion = f32[256,16,256]{0,2,1:T(8,128)S(1)} fusion(f32[256,16,256]{0,2,1:T(8,128)} %bitcast.16, pred[16,256]{1,0:T(8,128)(4,1)S(1)} %broadcast_in_dim.47), kind=kLoop, calls=%fused_computation.8 | loop fusion | flops 1048576 | bytes 8392704 | tf_op jit(solution)/shard_map/jit(_take)/select_n | solution.py:36
  43.5 55.5 %all_to_all.18 = f32[256,16,256]{0,2,1:T(8,128)} all-to-all(f32[256,16,256]{0,2,1:T(8,128)S(1)} %broadcast_select_fusion), channel_id=1, replica_groups=mesh['rows'=8,'bundle'=16] {'bundle'}, dimensions={1} | all-to-all | bytes 8388608 | tf_op jit(solution)/shard_map/all_to_all | solution.py:37
  99.0 2.5 stack.2
  101.5 9.1 %all-to-all-start.1 = ((f32[128,32,255]{2,1,0:T(8,128)}), f32[128,32,255]{2,1,0:T(8,128)}, u32[]{:S(2)}, u32[]{:S(2)}) async-start(f32[128,32,255]{2,1,0:T(8,128)} %stack.2), calls=%async_computation.1 | async-start | bytes 8388608 | tf_op jit(solution)/shard_map/all_to_all | solution.py:27
  110.7 1.7 gather_fusion.2
  112.5 5.3 %copy.10 = f32[16,256,256]{2,1,0:T(8,128)} copy(f32[16,256,256]{1,2,0:T(8,128)} %bitcast.17) | data formatting | bytes 8388608 | tf_op jit(solution)/shard_map/all_to_all | solution.py:37
  117.9 45.1 %all-to-all-done.1 = f32[128,32,255]{2,1,0:T(8,128)} async-done(((f32[128,32,255]{2,1,0:T(8,128)}), f32[128,32,255]{2,1,0:T(8,128)}, u32[]{:S(2)}, u32[]{:S(2)}) %all-to-all-start.1) | async-done | bytes 4177952 | tf_op jit(solution)/shard_map/all_to_all | solution.py:27
  163.0 3.2 gather_fusion.1
  166.4 145.1 %while.10 = (s32[]{:T(128)}, s32[8,512,256]{2,1,0:T(8,128)}, f32[8,512,256]{2,1,0:T(8,128)}, f32[256,255]{0,1:T(8,128)S(1)}, s32[]{:T(128)}) while((s32[]{:T(128)}, s32[8,512,256]{2,1,0:T(8,128)}, f32[8,512,256]{2,1,0:T(8,128)}, f32[256,255]{0,1:T(8,128)S(1)}, s32[]{:T(128)}) %tuple.23), condition=%wide.region_3.4_spmd, body=%wide.region_1.0_spmd.sunk | while | flops 100139008 | bytes 3407425 | solution.py:16
  166.4 1.1 dynamic-slice_bitcast_fusion.2
  167.5 16.2 %convert_reduce_fusion.2 = s32[512,256]{1,0:T(8,128)S(1)} fusion(f32[256,255]{0,1:T(8,128)S(1)} %get-tuple-element.80, f32[512,256]{1,0:T(8,128)S(1)} %dynamic-slice_bitcast_fusion.2), kind=kLoop, calls=%fused_computation.4.clone.1 | loop fusion | flops 100139008 | bytes 1309696 | tf_op jit(solution)/shard_map/while/body/eval_jaxpr/reduce_sum | solution.py:13
  185.6 16.2 %convert_reduce_fusion.2 = s32[512,256]{1,0:T(8,128)S(1)} fusion(f32[256,255]{0,1:T(8,128)S(1)} %get-tuple-element.80, f32[512,256]{1,0:T(8,128)S(1)} %dynamic-slice_bitcast_fusion.2), kind=kLoop, calls=%fused_computation.4.clone.1 | loop fusion | flops 100139008 | bytes 1309696 | tf_op jit(solution)/shard_map/while/body/eval_jaxpr/reduce_sum | solution.py:13
  203.8 16.2 %convert_reduce_fusion.2 = s32[512,256]{1,0:T(8,128)S(1)} fusion(f32[256,255]{0,1:T(8,128)S(1)} %get-tuple-element.80, f32[512,256]{1,0:T(8,128)S(1)} %dynamic-slice_bitcast_fusion.2), kind=kLoop, calls=%fused_computation.4.clone.1 | loop fusion | flops 100139008 | bytes 1309696 | tf_op jit(solution)/shard_map/while/body/eval_jaxpr/reduce_sum | solution.py:13
  221.9 16.2 %convert_reduce_fusion.2 = s32[512,256]{1,0:T(8,128)S(1)} fusion(f32[256,255]{0,1:T(8,128)S(1)} %get-tuple-element.80, f32[512,256]{1,0:T(8,128)S(1)} %dynamic-slice_bitcast_fusion.2), kind=kLoop, calls=%fused_computation.4.clone.1 | loop fusion | flops 100139008 | bytes 1309696 | tf_op jit(solution)/shard_map/while/body/eval_jaxpr/reduce_sum | solution.py:13
  240.1 16.2 %convert_reduce_fusion.2 = s32[512,256]{1,0:T(8,128)S(1)} fusion(f32[256,255]{0,1:T(8,128)S(1)} %get-tuple-element.80, f32[512,256]{1,0:T(8,128)S(1)} %dynamic-slice_bitcast_fusion.2), kind=kLoop, calls=%fused_computation.4.clone.1 | loop fusion | flops 100139008 | bytes 1309696 | tf_op jit(solution)/shard_map/while/body/eval_jaxpr/reduce_sum | solution.py:13
  257.1 1.1 dynamic-slice_bitcast_fusion.2
  258.2 16.2 %convert_reduce_fusion.2 = s32[512,256]{1,0:T(8,128)S(1)} fusion(f32[256,255]{0,1:T(8,128)S(1)} %get-tuple-element.80, f32[512,256]{1,0:T(8,128)S(1)} %dynamic-slice_bitcast_fusion.2), kind=kLoop, calls=%fused_computation.4.clone.1 | loop fusion | flops 100139008 | bytes 1309696 | tf_op jit(solution)/shard_map/while/body/eval_jaxpr/reduce_sum | solution.py:13
  275.3 1.1 dynamic-slice_bitcast_fusion.2
  276.3 16.2 %convert_reduce_fusion.2 = s32[512,256]{1,0:T(8,128)S(1)} fusion(f32[256,255]{0,1:T(8,128)S(1)} %get-tuple-element.80, f32[512,256]{1,0:T(8,128)S(1)} %dynamic-slice_bitcast_fusion.2), kind=kLoop, calls=%fused_computation.4.clone.1 | loop fusion | flops 100139008 | bytes 1309696 | tf_op jit(solution)/shard_map/while/body/eval_jaxpr/reduce_sum | solution.py:13
  294.5 16.2 %convert_reduce_fusion.2 = s32[512,256]{1,0:T(8,128)S(1)} fusion(f32[256,255]{0,1:T(8,128)S(1)} %get-tuple-element.80, f32[512,256]{1,0:T(8,128)S(1)} %dynamic-slice_bitcast_fusion.2), kind=kLoop, calls=%fused_computation.4.clone.1 | loop fusion | flops 100139008 | bytes 1309696 | tf_op jit(solution)/shard_map/while/body/eval_jaxpr/reduce_sum | solution.py:13
  311.5 4.5 %bitcast_add_fusion = s32[4096,256]{1,0:T(8,128)} fusion(s32[8,512,256]{2,1,0:T(8,128)} %get-tuple-element.27, s32[256]{0:T(256)S(1)} %get-tuple-element.40), kind=kLoop, calls=%fused_computation.7 | loop fusion | flops 1048576 | bytes 8389632 | tf_op jit(solution)/shard_map/add | solution.py:40
  (28 shorter events, 13.2 us)
Async XLA Ops:
  0.0 110.7 %copy-start = (s32[4096]{0:T(1024)S(1)}, s32[4096]{0:T(1024)}, u32[]{:S(2)}) copy-start(s32[4096]{0:T(1024)} %param.9) | copy-start | bytes 49156
  43.5 55.5 %copy-start.1 = (f32[32,255]{1,0:T(8,128)S(1)}, f32[32,255]{1,0:T(8,128)}, u32[]{:S(2)}) copy-start(f32[32,255]{1,0:T(8,128)} %param.7) | copy-start | bytes 97924
  101.5 61.5 %all-to-all-start.1 = ((f32[128,32,255]{2,1,0:T(8,128)}), f32[128,32,255]{2,1,0:T(8,128)}, u32[]{:S(2)}, u32[]{:S(2)}) async-start(f32[128,32,255]{2,1,0:T(8,128)} %stack.2), calls=%async_computation.1 | async-start | bytes 8388608 | tf_op jit(solution)/shard_map/all_to_all | solution.py:27
